TPU v7x, 32 devices: a whole 2x2x4 slice. The times are simulated.
32 devices in a mesh: shard: 16 (over z, y, x), mp: 2 (over core).
Axes of the slice: x: 2, y: 2, z: 4, core: 2. Of those that a mesh axis runs over, the one named last changes fastest.
Arguments:
- item_rows: float32 [4096, 256], P('shard', 'mp'), may hold values from -6 to 6
- first_moment: float32 [4096, 256], P('shard', 'mp'), may hold values from -2 to 2
- second_moment: float32 [4096, 256], P('shard', 'mp'), may hold values from 0.01 to 4
- item_cot: bfloat16 [4096, 256], P('shard', 'mp'), may hold values from -6 to 6
- tile_bits: int32 [256, 8, 128], P('shard'), may hold values from 0 to 65535, as said below
- tile_item: int32 [256], P('shard'), may hold values from 0 to 1
- tile_dest: int32 [256], P('shard'), may hold values from 0 to 15
- basket_gain: float32 [256], replicated, may hold values from 0.1 to 1.9
- item_gain: float32 [256], replicated, may hold values from 0.1 to 1.9
- gate_basket: bfloat16 [256, 2048], P(None, 'mp'), may hold values from -0.375 to 0.375
- up_basket: bfloat16 [256, 2048], P(None, 'mp'), may hold values from -0.375 to 0.375
- down_basket: bfloat16 [2048, 256], P('mp'), may hold values from -0.125 to 0.125
- gate_item: bfloat16 [256, 2048], P(None, 'mp'), may hold values from -0.375 to 0.375
- up_item: bfloat16 [256, 2048], P(None, 'mp'), may hold values from -0.375 to 0.375
- down_item: bfloat16 [2048, 256], P('mp'), may hold values from -0.125 to 0.125
Outputs:
- new_rows: float32 [4096, 256], P('shard', 'mp')
- new_first: float32 [4096, 256], P('shard', 'mp')
- new_second: float32 [4096, 256], P('shard', 'mp')
Inputs may be any that keep to these rules, and one draw needn't show every extreme that they name: `tile_bits`: each word holds 16 independent incidence bits in its low bits.
All inputs are finite; a program needn't handle non-finite values.
Results may differ from a plain program's by a relative error of at most 0.007.
Values may be sent and summed in bfloat16 or wider, within the bound.
No kernel may reach another device: no remote copies, remote signals or barrier semaphores. Data moves between devices by JAX's collectives and lax.ppermute only.
A program may use at most 128 MiB of HBM per device.

v0:
```python
import jax
import jax.numpy as jnp
from jax import lax
from jax.sharding import PartitionSpec as P

D = 256
BLOCK = 128
NORM_EPSILON = 1e-05
LEARNING_RATE = 0.01
BETA_FIRST = 0.9
BETA_SECOND = 0.99
ADAM_EPSILON = 1e-08


def unpack_tiles(packed):
    shifts = jnp.arange(16, dtype=jnp.int32)
    bit_values = jnp.right_shift(packed[:, :, None, :], shifts[None, None, :, None]) & 1
    return bit_values.reshape(packed.shape[0], packed.shape[1] * 16, packed.shape[2]).astype(
        jnp.bfloat16
    )


def silu_parts(gate_values):
    sigmoid = jax.nn.sigmoid(gate_values)
    return (gate_values * sigmoid, sigmoid * (1.0 + gate_values * (1.0 - sigmoid)))


def rms_scale(values):
    return lax.rsqrt(jnp.mean(values * values, axis=-1, keepdims=True) + NORM_EPSILON)


def owner_sums(partials, tile_dest):
    block_total = lax.axis_size("shard")
    coalesced = jax.ops.segment_sum(partials, tile_dest, num_segments=block_total)
    received = lax.all_to_all(
        coalesced.astype(jnp.bfloat16), "shard", split_axis=0, concat_axis=0, tiled=True
    ).astype(coalesced.dtype)
    return jnp.sum(received, axis=0)


def spread_items(owned, masks, tile_item, tile_dest, item_blocks):
    gathered = lax.all_gather(owned, "shard", axis=0, tiled=True)
    gathered = gathered.reshape(-1, BLOCK, owned.shape[1])
    selected = jnp.take(gathered, tile_dest, axis=0)
    contrib = jnp.einsum("tib,tbf->tif", masks, selected, preferred_element_type=jnp.float32)
    summed = jax.ops.segment_sum(contrib, tile_item, num_segments=item_blocks)
    return summed.reshape(item_blocks * BLOCK, owned.shape[1])


def whole_features(values):
    return lax.all_gather(values.astype(jnp.bfloat16), "mp", axis=1, tiled=True).astype(
        values.dtype
    )


def local(
    item_rows,
    first_moment,
    second_moment,
    item_cot,
    tile_bits,
    tile_item,
    tile_dest,
    basket_gain,
    item_gain,
    gate_basket,
    up_basket,
    down_basket,
    gate_item,
    up_item,
    down_item,
):
    half_width = item_rows.shape[1]
    item_blocks = item_rows.shape[0] // BLOCK
    offset = lax.axis_index("mp") * half_width
    masks = unpack_tiles(tile_bits)
    rows_blocks = item_rows.astype(jnp.bfloat16).reshape(item_blocks, BLOCK, half_width)
    picked = jnp.take(rows_blocks, tile_item, axis=0)
    partials = jnp.einsum("tib,tif->tbf", masks, picked, preferred_element_type=jnp.float32)
    basket_sum = owner_sums(partials, tile_dest)
    sum_full = whole_features(basket_sum)
    scale_basket = rms_scale(sum_full)
    normed = sum_full * scale_basket * basket_gain
    normed_bf = normed.astype(jnp.bfloat16)
    gate_pre = jnp.dot(normed_bf, gate_basket, preferred_element_type=jnp.float32)
    up_pre = jnp.dot(normed_bf, up_basket, preferred_element_type=jnp.float32)
    silu_value, silu_slope = silu_parts(gate_pre)
    hidden = (silu_value * up_pre).astype(jnp.bfloat16)
    down_part = jnp.dot(hidden, down_basket, preferred_element_type=jnp.float32)
    down_mine = lax.psum_scatter(
        down_part.astype(jnp.bfloat16), "mp", scatter_dimension=1, tiled=True
    ).astype(jnp.float32)
    basket_out = (lax.dynamic_slice_in_dim(normed, offset, half_width, 1) + down_mine).astype(
        jnp.bfloat16
    )
    message = spread_items(basket_out, masks, tile_item, tile_dest, item_blocks)
    message_full = lax.all_gather(message, "mp", axis=1, tiled=True)
    scale_item = rms_scale(message_full)
    query = (message_full * scale_item * item_gain).astype(jnp.bfloat16)
    gate_item_pre = jnp.dot(query, gate_item, preferred_element_type=jnp.float32)
    up_item_pre = jnp.dot(query, up_item, preferred_element_type=jnp.float32)
    item_value, item_slope = silu_parts(gate_item_pre)
    cot_full = lax.all_gather(item_cot, "mp", axis=1, tiled=True)
    grad_hidden = jnp.einsum("rd,hd->rh", cot_full, down_item, preferred_element_type=jnp.float32)
    grad_up = (grad_hidden * item_value).astype(jnp.bfloat16)
    grad_gate = (grad_hidden * up_item_pre * item_slope).astype(jnp.bfloat16)
    query_part = jnp.einsum(
        "rh,dh->rd", grad_gate, gate_item, preferred_element_type=jnp.float32
    ) + jnp.einsum("rh,dh->rd", grad_up, up_item, preferred_element_type=jnp.float32)
    gain_mine = lax.dynamic_slice_in_dim(item_gain, offset, half_width, 0)
    grad_query = lax.psum_scatter(
        query_part.astype(jnp.bfloat16), "mp", scatter_dimension=1, tiled=True
    ).astype(jnp.float32)
    inner = lax.psum(jnp.sum(gain_mine * grad_query * message, axis=1, keepdims=True), "mp")
    cubed_item = scale_item * scale_item * scale_item
    grad_message = (scale_item * gain_mine * grad_query - message * cubed_item * inner / D).astype(
        jnp.bfloat16
    )
    grad_blocks = grad_message.reshape(item_blocks, BLOCK, half_width)
    grad_picked = jnp.take(grad_blocks, tile_item, axis=0)
    grad_partials = jnp.einsum(
        "tib,tif->tbf", masks, grad_picked, preferred_element_type=jnp.float32
    )
    grad_out = owner_sums(grad_partials, tile_dest)
    grad_out_full = whole_features(grad_out)
    grad_out_bf = grad_out_full.astype(jnp.bfloat16)
    grad_basket_hidden = jnp.einsum(
        "bd,hd->bh", grad_out_bf, down_basket, preferred_element_type=jnp.float32
    )
    grad_basket_up = (grad_basket_hidden * silu_value).astype(jnp.bfloat16)
    grad_basket_gate = (grad_basket_hidden * up_pre * silu_slope).astype(jnp.bfloat16)
    normed_part = jnp.einsum(
        "bh,dh->bd", grad_basket_gate, gate_basket, preferred_element_type=jnp.float32
    ) + jnp.einsum("bh,dh->bd", grad_basket_up, up_basket, preferred_element_type=jnp.float32)
    grad_normed = grad_out_full + lax.psum(normed_part.astype(jnp.bfloat16), "mp").astype(
        jnp.float32
    )
    inner_basket = jnp.sum(basket_gain * grad_normed * sum_full, axis=1, keepdims=True)
    cubed_basket = scale_basket * scale_basket * scale_basket
    grad_sum = scale_basket * basket_gain * grad_normed - sum_full * cubed_basket * inner_basket / D
    grad_sum_mine = lax.dynamic_slice_in_dim(grad_sum, offset, half_width, 1).astype(jnp.bfloat16)
    back_items = spread_items(grad_sum_mine, masks, tile_item, tile_dest, item_blocks)
    gradient = item_cot.astype(jnp.float32) + back_items
    new_first = BETA_FIRST * first_moment + (1.0 - BETA_FIRST) * gradient
    new_second = BETA_SECOND * second_moment + (1.0 - BETA_SECOND) * gradient * gradient
    new_rows = item_rows - LEARNING_RATE * new_first / (jnp.sqrt(new_second) + ADAM_EPSILON)
    return (new_rows, new_first, new_second)


def solution(mesh):
    return jax.shard_map(
        local,
        mesh=mesh,
        in_specs=(
            P("shard", "mp"),
            P("shard", "mp"),
            P("shard", "mp"),
            P("shard", "mp"),
            P("shard", None, None),
            P("shard"),
            P("shard"),
            P(),
            P(),
            P(None, "mp"),
            P(None, "mp"),
            P("mp", None),
            P(None, "mp"),
            P(None, "mp"),
            P("mp", None),
        ),
        out_specs=(P("shard", "mp"), P("shard", "mp"), P("shard", "mp")),
        check_vma=False,
    )
```

profile of v0, /device:TPU:0, one launch (start us, length us, event | category | flops | bytes accessed | tf_op | source)
XLA Modules:
  0.0 214.6 jit_solution(4999208334677294689)
XLA Ops:
  7.2 0.7 compare_select_fusion.1
  8.0 0.9 convert_element_type.76
  10.9 1.6 scatter_fusion
  12.5 0.9 convert_element_type.77
  13.4 8.5 %all-to-all-start = ((bf16[16,128,128]{2,1,0:T(8,128)(2,1)}), bf16[16,128,128]{2,1,0:T(8,128)(2,1)S(1)}, u32[]{:S(2)}, u32[]{:S(2)}) async-start(bf16[16,128,128]{2,1,0:T(8,128)(2,1)} %convert_element_type.77), calls=%async_computation | async-start | bytes 1048576 | tf_op jit(solution)/shard_map/all_to_all | solution.py:35
  22.0 1.9 all_gather.21
  24.0 1.3 fusion.56
  25.3 11.7 %all-to-all-done = bf16[16,128,128]{2,1,0:T(8,128)(2,1)S(1)} async-done(((bf16[16,128,128]{2,1,0:T(8,128)(2,1)}), bf16[16,128,128]{2,1,0:T(8,128)(2,1)S(1)}, u32[]{:S(2)}, u32[]{:S(2)}) %all-to-all-start) | async-done | bytes 524320 | tf_op jit(solution)/shard_map/all_to_all | solution.py:35
  37.1 1.9 all_gather.18
  40.1 0.8 copy-done.3
  41.6 0.8 copy-done.7
  42.7 0.7 copy.26
  43.6 5.9 %reduce-scatter.7.cloned.1.call-done = bf16[128,128]{1,0:T(8,128)(2,1)} async-done(((bf16[256,128]{1,0:T(8,128)(2,1)}), bf16[128,128]{1,0:T(8,128)(2,1)}) %reduce-scatter.7.cloned.1.call-update) | async-done | bytes 32784
  49.5 0.9 copy.27
  50.4 44.0 %all_gather.19 = bf16[2048,128]{1,0:T(8,128)(2,1)S(1)} all-gather(bf16[128,128]{1,0:T(8,128)(2,1)S(1)} %add_convert_fusion), channel_id=1, replica_groups=mesh['shard'=16,'mp'=2] {'shard'}, dimensions={0}, use_global_device_ids=true | all-gather | bytes 557056 | tf_op jit(solution)/shard_map/all_gather | solution.py:42
  95.4 1.6 scatter_fusion.1
  97.0 2.0 all_gather.20
  100.9 2.0 fusion.2
  102.9 1.7 fusion.3
  104.6 0.8 copy.28
  105.5 3.5 %reduce-scatter.9.cloned.1.call-done = bf16[128,256]{1,0:T(8,128)(2,1)} async-done(((bf16[256,256]{1,0:T(8,128)(2,1)}), bf16[128,256]{1,0:T(8,128)(2,1)}) %reduce-scatter.9.cloned.1.call-update) | async-done | bytes 65552
  109.0 0.9 copy.29
  110.1 2.5 %psum.14 = f32[256]{0:T(256)S(1)} all-reduce(f32[256]{0:T(256)S(1)} %fusion.33), channel_id=1, replica_groups=mesh['shard'=16,'mp'=2] {'mp'}, use_global_device_ids=true, to_apply=%region_8.11 | all-reduce | flops 256 | bytes 2048 | tf_op jit(solution)/shard_map/psum | solution.py:114
  113.9 1.6 scatter_fusion.2
  115.6 22.2 %all_to_all.10 = bf16[16,128,128]{2,1,0:T(8,128)(2,1)S(1)} all-to-all(bf16[16,128,128]{2,1,0:T(8,128)(2,1)S(1)} %convert_element_type.90), channel_id=1, replica_groups=mesh['shard'=16,'mp'=2] {'shard'}, dimensions={0} | all-to-all | bytes 1048576 | tf_op jit(solution)/shard_map/all_to_all | solution.py:35
  137.8 2.0 all_gather.22
  142.1 1.0 fusion.4
  143.2 16.2 %all-reduce.2.cloned.1.call-done = bf16[128,256]{1,0:T(8,128)(2,1)} async-done(((bf16[128,256]{1,0:T(8,128)(2,1)}), bf16[128,256]{1,0:T(8,128)(2,1)}) %all-reduce.2.cloned.1.call-update) | async-done | bytes 65552 | tf_op jit(solution)/shard_map/psum | solution.py:135
  159.4 1.0 multiply_reduce_fusion.1
  160.5 44.1 %all_gather.23 = bf16[2048,128]{1,0:T(8,128)(2,1)S(1)} all-gather(bf16[128,128]{1,0:T(8,128)(2,1)S(1)} %fusion.38), channel_id=1, replica_groups=mesh['shard'=16,'mp'=2] {'shard'}, dimensions={0}, use_global_device_ids=true | all-gather | bytes 557056 | tf_op jit(solution)/shard_map/all_gather | solution.py:42
  205.7 1.6 scatter_fusion.3
  207.3 0.8 divide_subtract_fusion
  (89 shorter events, 12.5 us)
Async XLA Ops:
  7.2 92.0 %copy-start = (bf16[256,1024]{1,0:T(8,128)(2,1)S(1)}, bf16[256,1024]{1,0:T(8,128)(2,1)}, u32[]{:S(2)}) copy-start(bf16[256,1024]{1,0:T(8,128)(2,1)} %param.31) | copy-start | bytes 1572868
  7.2 0.7 copy-start.19
  8.0 1.0 copy-start.16
  10.3 0.7 copy-start.18
  13.4 8.5 %copy-start.13 = (bf16[256,128]{1,0:T(8,128)(2,1)S(1)}, bf16[256,128]{1,0:T(8,128)(2,1)}, u32[]{:S(2)}) copy-start(bf16[256,128]{1,0:T(8,128)(2,1)} %param.22) | copy-start | bytes 196612
  13.4 10.5 %copy-start.10 = (bf16[1024,256]{1,0:T(8,128)(2,1)S(1)}, bf16[1024,256]{1,0:T(8,128)(2,1)}, u32[]{:S(2)}) copy-start(bf16[1024,256]{1,0:T(8,128)(2,1)} %param.33) | copy-start | bytes 1572868
  13.4 23.6 %all-to-all-start = ((bf16[16,128,128]{2,1,0:T(8,128)(2,1)}), bf16[16,128,128]{2,1,0:T(8,128)(2,1)S(1)}, u32[]{:S(2)}, u32[]{:S(2)}) async-start(bf16[16,128,128]{2,1,0:T(8,128)(2,1)} %convert_element_type.77), calls=%async_computation | async-start | bytes 1048576 | tf_op jit(solution)/shard_map/all_to_all | solution.py:35
  21.9 27.6 %reduce-scatter.7.cloned.1.call-start = ((), (), s32[]{:S(2)}) async-start(), calls=%async_computation.5 | async-start | bytes 98304
  25.3 13.8 %copy-start.1 = (bf16[256,1024]{1,0:T(8,128)(2,1)S(1)}, bf16[256,1024]{1,0:T(8,128)(2,1)}, u32[]{:S(2)}) copy-start(bf16[256,1024]{1,0:T(8,128)(2,1)} %param.28) | copy-start | bytes 1572868
  39.1 0.7 copy-start.17
  39.8 1.0 copy-start.3
  40.8 0.8 copy-start.5
  40.8 1.6 copy-start.11
  41.6 0.8 copy-start.7
  43.5 65.5 %reduce-scatter.9.cloned.1.call-start = ((), (), s32[]{:S(2)}) async-start(), calls=%async_computation.6 | async-start | bytes 196608
  99.2 0.7 copy-start.20
  99.8 1.0 copy-start.21
  105.3 54.1 %all-reduce.2.cloned.1.call-start = ((), (), s32[]{:S(2)}) async-start(), calls=%async_computation.4 | async-start | bytes 131072 | tf_op jit(solution)/shard_map/psum | solution.py:135
  115.6 24.3 %copy-start.12 = (bf16[1024,256]{1,0:T(8,128)(2,1)S(1)}, bf16[1024,256]{1,0:T(8,128)(2,1)}, u32[]{:S(2)}) copy-start(bf16[1024,256]{1,0:T(8,128)(2,1)} %param.30) | copy-start | bytes 1572868
  137.8 2.4 %copy-start.8 = (f32[128,1024]{1,0:T(8,128)S(1)}, f32[128,1024]{1,0:T(8,128)}, u32[]{:S(2)}) copy-start(f32[128,1024]{1,0:T(8,128)} %copy-done.7) | copy-start | bytes 1572868
  139.9 1.0 copy-start.2
  139.9 1.2 copy-start.6
  141.1 1.0 copy-start.4
  205.6 1.6 copy-start.9
  205.6 1.6 copy-start.14
  205.6 1.6 copy-start.15
Sparse Core Ops, SparseCore 0:
  43.6 5.8 reduce-scatter.6
  105.5 3.4 reduce-scatter.8
  143.2 16.1 all-reduce.1
where the time goes:
time: 215 us
  blocking collectives  121 us (56%)
  waiting for transfers between devices  37.4 us (17%)
  between operations  14.2 us (7%)
  local copies, waits for them, and re-layouts  12.6 us (6%)
  other arithmetic  12 us (6%)
  matrix products  9.28 us (4%)
  starting transfers between devices  8.6 us (4%)
    all_gather x2, blocking collectives, spread_items(): gathered = lax.all_gather(owned, 'shard', axis=0, tiled=True)  88 us
    all_to_all x1, blocking collectives, owner_sums(): lax.all_to_all(coalesced.astype(jnp.bfloat16), 'shard', split_axis=0, con...  22.2 us
    psum x1, waiting for transfers between devices, local(): lax.psum(normed_part.astype(jnp.bfloat16), 'mp').astype(jnp.float32)  16.2 us
    all_to_all x1, waiting for transfers between devices, owner_sums(): lax.all_to_all(coalesced.astype(jnp.bfloat16), 'shard', split_axis=0, con...  11.7 us
    unnamed x48, local copies, waits for them, and re-layouts  9.61 us
    unnamed x5, waiting for transfers between devices  9.45 us
    all_to_all x1, starting transfers between devices, owner_sums(): lax.all_to_all(coalesced.astype(jnp.bfloat16), 'shard', split_axis=0, con...  8.47 us
  transfers between devices with their start and end apart: 4, of which 4 were waited for; matrix products, arithmetic and copies ran while one was open for 1% of the time, Pallas kernels for 0%

commit v1 on v0

--- a/solution.py
+++ b/solution.py
@@ -10,6 +10,11 @@
 BETA_FIRST = 0.9
 BETA_SECOND = 0.99
 ADAM_EPSILON = 1e-08
+
+
+def gather_and_add(value, name):
+    blocks = lax.all_gather(value, name)
+    return jnp.sum(blocks, axis=0)
 
 
 def unpack_tiles(packed):
@@ -132,7 +137,7 @@
     normed_part = jnp.einsum(
         "bh,dh->bd", grad_basket_gate, gate_basket, preferred_element_type=jnp.float32
     ) + jnp.einsum("bh,dh->bd", grad_basket_up, up_basket, preferred_element_type=jnp.float32)
-    grad_normed = grad_out_full + lax.psum(normed_part.astype(jnp.bfloat16), "mp").astype(
+    grad_normed = grad_out_full + gather_and_add(normed_part.astype(jnp.bfloat16), "mp").astype(
         jnp.float32
     )
     inner_basket = jnp.sum(basket_gain * grad_normed * sum_full, axis=1, keepdims=True)

time: 215 us -> 198 us (0.921)
  blocking collectives: 121 us -> 97.4 us
  starting transfers between devices: 8.6 us -> 15.4 us
    all_to_all x1 -> x0, blocking collectives: 22.2 us -> none  [owner_sums(): lax.all_to_all(coalesced.astype(jnp.bfloat16), 'shard', split_axis=0, con...]
    psum x1 -> x0, waiting for transfers between devices: 16.2 us -> none  [local(): lax.psum(normed_part.astype(jnp.bfloat16), 'mp').astype(jnp.float32)]
    all_to_all x1 -> x2, waiting for transfers between devices: 11.7 us -> 27.1 us  [owner_sums(): lax.all_to_all(coalesced.astype(jnp.bfloat16), 'shard', split_axis=0, con...]
    all_to_all x1 -> x2, starting transfers between devices: 8.47 us -> 15.4 us  [owner_sums(): lax.all_to_all(coalesced.astype(jnp.bfloat16), 'shard', split_axis=0, con...]
    all_gather x2, blocking collectives: 88 us -> 85.2 us  [spread_items(): gathered = lax.all_gather(owned, 'shard', axis=0, tiled=True)]
    unnamed x5 -> x4, waiting for transfers between devices: 9.45 us -> 9.49 us
where the time goes in v1:
time: 198 us; the launch traced here: 197 us
  blocking collectives  97.4 us (49%)
  waiting for transfers between devices  36.6 us (18%)
  starting transfers between devices  15.4 us (8%)
  between operations  14.5 us (7%)
  local copies, waits for them, and re-layouts  12.6 us (6%)
  other arithmetic  12 us (6%)
  matrix products  8.64 us (4%)
    all_gather x2, blocking collectives, spread_items(): gathered = lax.all_gather(owned, 'shard', axis=0, tiled=True)  85.2 us
    all_to_all x2, waiting for transfers between devices, owner_sums(): lax.all_to_all(coalesced.astype(jnp.bfloat16), 'shard', split_axis=0, con...  27.1 us
    all_to_all x2, starting transfers between devices, owner_sums(): lax.all_to_all(coalesced.astype(jnp.bfloat16), 'shard', split_axis=0, con...  15.4 us
    unnamed x48, local copies, waits for them, and re-layouts  9.6 us
    unnamed x4, waiting for transfers between devices  9.49 us
  transfers between devices with their start and end apart: 4, of which 4 were waited for; matrix products, arithmetic and copies ran while one was open for 1% of the time, Pallas kernels for 0%

profile of v1, /device:TPU:0, one launch (start us, length us, event | category | flops | bytes accessed | tf_op | source)
XLA Modules:
  0.0 197.2 jit_solution(12847813538910238706)
XLA Ops:
  7.2 0.7 compare_select_fusion.1
  8.0 0.9 convert_element_type.78
  10.9 1.6 scatter_fusion
  12.5 0.9 convert_element_type.79
  13.4 8.5 %all-to-all-start = ((bf16[16,128,128]{2,1,0:T(8,128)(2,1)}), bf16[16,128,128]{2,1,0:T(8,128)(2,1)S(1)}, u32[]{:S(2)}, u32[]{:S(2)}) async-start(bf16[16,128,128]{2,1,0:T(8,128)(2,1)} %convert_element_type.79), calls=%async_computation | async-start | bytes 1048576 | tf_op jit(solution)/shard_map/all_to_all | solution.py:40
  22.0 1.9 all_gather.27
  24.0 1.3 fusion.56
  25.3 11.7 %all-to-all-done = bf16[16,128,128]{2,1,0:T(8,128)(2,1)S(1)} async-done(((bf16[16,128,128]{2,1,0:T(8,128)(2,1)}), bf16[16,128,128]{2,1,0:T(8,128)(2,1)S(1)}, u32[]{:S(2)}, u32[]{:S(2)}) %all-to-all-start) | async-done | bytes 524320 | tf_op jit(solution)/shard_map/all_to_all | solution.py:40
  37.1 1.9 all_gather.24
  40.1 0.8 copy-done.3
  41.6 0.8 copy-done.7
  42.7 0.7 copy.26
  43.6 5.9 %reduce-scatter.7.cloned.1.call-done = bf16[128,128]{1,0:T(8,128)(2,1)} async-done(((bf16[256,128]{1,0:T(8,128)(2,1)}), bf16[128,128]{1,0:T(8,128)(2,1)}) %reduce-scatter.7.cloned.1.call-update) | async-done | bytes 32784
  49.5 0.9 copy.27
  50.4 44.0 %all_gather.25 = bf16[2048,128]{1,0:T(8,128)(2,1)S(1)} all-gather(bf16[128,128]{1,0:T(8,128)(2,1)S(1)} %add_convert_fusion), channel_id=1, replica_groups=mesh['shard'=16,'mp'=2] {'shard'}, dimensions={0}, use_global_device_ids=true | all-gather | bytes 557056 | tf_op jit(solution)/shard_map/all_gather | solution.py:47
  95.4 1.6 scatter_fusion.1
  97.0 2.0 %all_gather.26 = f32[256,256]{1,0:T(8,128)S(1)} all-gather(f32[256,128]{1,0:T(8,128)S(1)} %bitcast.43), channel_id=1, replica_groups=mesh['shard'=16,'mp'=2] {'mp'}, dimensions={1}, use_global_device_ids=true | all-gather | bytes 393216 | tf_op jit(solution)/shard_map/all_gather | solution.py:102
  100.9 2.0 %fusion.2 = f32[256,256]{1,0:T(8,128)S(1)} fusion(bf16[256,1024]{1,0:T(8,128)(2,1)S(1)} %copy-done, f32[256,1024]{1,0:T(8,128)} %fusion.56, bf16[256,1024]{1,0:T(8,128)(2,1)S(1)} %copy-done.21, f32[256,1024]{1,0:T(8,128)S(1)} %fusion.54, f32[256,256]{1,0:T(8,128)S(1)} %all_gather.26, f32[256]{0:T(256)S(1)} %copy-done.20, f32[256]{0:T(256)S(1)} %get-tuple-element.11), kind=kOutput, calls=%fused_computation.11 | convolution fusion | flops 271253504 | bytes 3672064 | tf_op jit(solution)/shard_map/rh,dh->rd/dot_general | solution.py:112
  102.9 1.7 fusion.3
  104.6 0.8 copy.28
  105.4 3.6 %reduce-scatter.9.cloned.1.call-done = bf16[128,256]{1,0:T(8,128)(2,1)} async-done(((bf16[256,256]{1,0:T(8,128)(2,1)}), bf16[128,256]{1,0:T(8,128)(2,1)}) %reduce-scatter.9.cloned.1.call-update) | async-done | bytes 65552
  109.0 0.9 copy.29
  110.1 2.5 %psum.7 = f32[256]{0:T(256)S(1)} all-reduce(f32[256]{0:T(256)S(1)} %fusion.33), channel_id=1, replica_groups=mesh['shard'=16,'mp'=2] {'mp'}, use_global_device_ids=true, to_apply=%region_8.11 | all-reduce | flops 256 | bytes 2048 | tf_op jit(solution)/shard_map/psum | solution.py:119
  113.9 1.6 scatter_fusion.2
  115.5 0.9 convert_element_type.92
  116.4 6.9 %all-to-all-start.1 = ((bf16[16,128,128]{2,1,0:T(8,128)(2,1)}), bf16[16,128,128]{2,1,0:T(8,128)(2,1)S(1)}, u32[]{:S(2)}, u32[]{:S(2)}) async-start(bf16[16,128,128]{2,1,0:T(8,128)(2,1)} %convert_element_type.92), calls=%async_computation.1 | async-start | bytes 1048576 | tf_op jit(solution)/shard_map/all_to_all | solution.py:40
  123.3 15.4 %all-to-all-done.1 = bf16[16,128,128]{2,1,0:T(8,128)(2,1)S(1)} async-done(((bf16[16,128,128]{2,1,0:T(8,128)(2,1)}), bf16[16,128,128]{2,1,0:T(8,128)(2,1)S(1)}, u32[]{:S(2)}, u32[]{:S(2)}) %all-to-all-start.1) | async-done | bytes 524320 | tf_op jit(solution)/shard_map/all_to_all | solution.py:40
  138.8 2.0 %all_gather.28 = bf16[128,256]{1,0:T(8,128)(2,1)S(1)} all-gather(bf16[128,128]{1,0:T(8,128)(2,1)S(1)} %reduce_sum.76), channel_id=1, replica_groups=mesh['shard'=16,'mp'=2] {'mp'}, dimensions={1}, use_global_device_ids=true | all-gather | bytes 98304 | tf_op jit(solution)/shard_map/all_gather | solution.py:56
  143.4 1.9 all-gather
  145.6 41.2 %all_gather.31 = bf16[2048,128]{1,0:T(8,128)(2,1)S(1)} all-gather(bf16[128,128]{1,0:T(8,128)(2,1)S(1)} %fusion.38), channel_id=1, replica_groups=mesh['shard'=16,'mp'=2] {'shard'}, dimensions={0}, use_global_device_ids=true | all-gather | bytes 557056 | tf_op jit(solution)/shard_map/all_gather | solution.py:47
  187.9 1.6 scatter_fusion.3
  189.5 0.8 divide_subtract_fusion
  (89 shorter events, 12.9 us)
Async XLA Ops:
  7.2 92.0 %copy-start = (bf16[256,1024]{1,0:T(8,128)(2,1)S(1)}, bf16[256,1024]{1,0:T(8,128)(2,1)}, u32[]{:S(2)}) copy-start(bf16[256,1024]{1,0:T(8,128)(2,1)} %param.31) | copy-start | bytes 1572868
  7.2 0.7 copy-start.19
  8.0 1.0 copy-start.16
  10.3 0.7 copy-start.18
  13.4 8.5 %copy-start.13 = (bf16[256,128]{1,0:T(8,128)(2,1)S(1)}, bf16[256,128]{1,0:T(8,128)(2,1)}, u32[]{:S(2)}) copy-start(bf16[256,128]{1,0:T(8,128)(2,1)} %param.22) | copy-start | bytes 196612
  13.4 10.5 %copy-start.10 = (bf16[1024,256]{1,0:T(8,128)(2,1)S(1)}, bf16[1024,256]{1,0:T(8,128)(2,1)}, u32[]{:S(2)}) copy-start(bf16[1024,256]{1,0:T(8,128)(2,1)} %param.33) | copy-start | bytes 1572868
  13.4 23.6 %all-to-all-start = ((bf16[16,128,128]{2,1,0:T(8,128)(2,1)}), bf16[16,128,128]{2,1,0:T(8,128)(2,1)S(1)}, u32[]{:S(2)}, u32[]{:S(2)}) async-start(bf16[16,128,128]{2,1,0:T(8,128)(2,1)} %convert_element_type.79), calls=%async_computation | async-start | bytes 1048576 | tf_op jit(solution)/shard_map/all_to_all | solution.py:40
  21.9 27.6 %reduce-scatter.7.cloned.1.call-start = ((), (), s32[]{:S(2)}) async-start(), calls=%async_computation.4 | async-start | bytes 98304
  25.3 13.8 %copy-start.1 = (bf16[256,1024]{1,0:T(8,128)(2,1)S(1)}, bf16[256,1024]{1,0:T(8,128)(2,1)}, u32[]{:S(2)}) copy-start(bf16[256,1024]{1,0:T(8,128)(2,1)} %param.28) | copy-start | bytes 1572868
  39.1 0.7 copy-start.17
  39.8 1.0 copy-start.3
  40.8 0.8 copy-start.5
  40.8 1.6 copy-start.11
  41.6 0.8 copy-start.7
  43.5 65.5 %reduce-scatter.9.cloned.1.call-start = ((), (), s32[]{:S(2)}) async-start(), calls=%async_computation.5 | async-start | bytes 196608
  99.2 0.7 copy-start.20
  99.8 1.0 copy-start.21
  116.4 24.5 %copy-start.12 = (bf16[1024,256]{1,0:T(8,128)(2,1)S(1)}, bf16[1024,256]{1,0:T(8,128)(2,1)}, u32[]{:S(2)}) copy-start(bf16[1024,256]{1,0:T(8,128)(2,1)} %param.30) | copy-start | bytes 1572868
  116.4 22.4 %all-to-all-start.1 = ((bf16[16,128,128]{2,1,0:T(8,128)(2,1)}), bf16[16,128,128]{2,1,0:T(8,128)(2,1)S(1)}, u32[]{:S(2)}, u32[]{:S(2)}) async-start(bf16[16,128,128]{2,1,0:T(8,128)(2,1)} %convert_element_type.92), calls=%async_computation.1 | async-start | bytes 1048576 | tf_op jit(solution)/shard_map/all_to_all | solution.py:40
  138.7 2.4 %copy-start.8 = (f32[128,1024]{1,0:T(8,128)S(1)}, f32[128,1024]{1,0:T(8,128)}, u32[]{:S(2)}) copy-start(f32[128,1024]{1,0:T(8,128)} %copy-done.7) | copy-start | bytes 1572868
  140.8 1.0 copy-start.2
  140.8 1.2 copy-start.6
  142.0 1.0 copy-start.4
  187.9 1.6 copy-start.9
  187.9 1.6 copy-start.14
  187.9 1.6 copy-start.15
Sparse Core Ops, SparseCore 0:
  43.6 5.8 reduce-scatter.6
  105.5 3.4 reduce-scatter.8
